TPU v7x, 512 devices: a 4x2x32 block of a 4x8x32 slice. The times are simulated.
512 devices in a mesh: groups: 2 (over y), ep: 32 (over z), tp: 4 (over x), sub: 2 (over core).
Axes of the slice: x: 4, y: 2, z: 32, core: 2. Of those that a mesh axis runs over, the one named last changes fastest.
The devices are a block of a 4x8x32 slice.
Arguments:
- queries: bfloat16 [1024, 64, 128], P(('groups', 'ep', 'sub'), 'tp'), parts along dimension 0, may hold values from -80 to 80
- new_keys: bfloat16 [1024, 4, 128], P(('groups', 'ep', 'sub'), 'tp'), parts along dimension 0, may hold values from -4 to 4
- new_values: bfloat16 [1024, 4, 128], P(('groups', 'ep', 'sub'), 'tp'), parts along dimension 0, may hold values from -5 to 5
- key_codes: int32 [1024, 4, 8, 128], P(('groups', 'ep', 'sub'), 'tp'), parts along dimension 0, may hold values from -2147483648 to 2147483647, as said below
- key_scale: bfloat16 [1024, 4, 4, 128], P(('groups', 'ep', 'sub'), 'tp'), parts along dimension 0, may hold values from 0.19921875 to 1
- key_zero: bfloat16 [1024, 4, 4, 128], P(('groups', 'ep', 'sub'), 'tp'), parts along dimension 0, may hold values from -1.5 to 0.5
- value_codes: int32 [1024, 4, 8, 128], P(('groups', 'ep', 'sub'), 'tp'), parts along dimension 0, may hold values from -2147483648 to 2147483647, as said below
- value_scale: bfloat16 [1024, 4, 128], P(('groups', 'ep', 'sub'), 'tp'), parts along dimension 0, may hold values from 0.19921875 to 1
- value_zero: bfloat16 [1024, 4, 128], P(('groups', 'ep', 'sub'), 'tp'), parts along dimension 0, may hold values from -1.1953125 to 0.19921875
- lengths: int32 [1024], P(('groups', 'ep', 'sub')), parts along dimension 0, may hold values from 1 to 128, as said below
- out_weight: bfloat16 [8192, 2048], P('tp', ('ep', 'sub')), may hold values from -0.0625 to 0.0625
- residual: bfloat16 [1024, 2048], P(('groups', 'ep', 'sub'), 'tp'), parts along dimension 0, may hold values from -8 to 8
- norm_gain: bfloat16 [2048], P('tp'), may hold values from 0.099609375 to 1.8984375
- expert_ids: int32 [1024, 8], P(('groups', 'ep', 'sub')), parts along dimension 0, may hold values from 0 to 63, all different within a row; in each aligned block of 8 rows (0 to 7, 8 to 15, ...) at most 2 rows name the same one
- route_weights: int32 [1024, 8], P(('groups', 'ep', 'sub')), parts along dimension 0, may hold values from 1 to 65535
- capacity: int32 [128], P('groups'), parts along dimension 0, may hold values from 16 to 32, as said below
- w_gate: bfloat16 [64, 2048, 768], P(('ep', 'sub'), 'tp'), may hold values from -0.125 to 0.125
- w_up: bfloat16 [64, 2048, 768], P(('ep', 'sub'), 'tp'), may hold values from -0.125 to 0.125
- w_down: bfloat16 [64, 768, 2048], P(('ep', 'sub'), None, 'tp'), may hold values from -0.21875 to 0.21875
Outputs:
- mixed: bfloat16 [1024, 2048], P(('groups', 'ep', 'sub'), 'tp'), parts along dimension 0
There are 2 independent parts, one for each index of `groups`. A program takes and returns all parts, laid end to end along the dimension named above; an argument that names none is the same for every part. Nothing has to cross between parts.
Inputs may be any that keep to these rules, and one draw needn't show every extreme that they name: `key_codes`: each word holds 16 two-bit codes: position 16 w + j in bits 2 j and 2 j + 1 of word w. `value_codes`: packed as key_codes. `lengths`: some request of the batch has exactly 128 cached positions. `expert_ids`: each row names 8 different experts; within the rows of one device (aligned blocks of 8 rows) no expert is named by more than 2 rows, and that bound is reached. Several experts have capacity 32.
All inputs are finite; a program needn't handle non-finite values.
Results may differ from a plain program's by a relative error of at most 0.014.
Values may be sent and summed in bfloat16 or wider, within the bound.
A program may use at most 64 MiB of HBM per device.

v0:
```python
import math

import jax
import jax.numpy as jnp
from jax import lax
from jax.sharding import PartitionSpec as P

EPS = 1e-06


def in_order(parts, dim):
    parts = jnp.moveaxis(parts, 0, dim)
    lengths = parts.shape
    return parts.reshape(*lengths[:dim], lengths[dim] * lengths[dim + 1], *lengths[dim + 2 :])


def stacked_from(value, axes, order):
    parts = value
    for k in order:
        parts = lax.all_gather(parts, axes[k])
    done = order[::-1]
    back = [done.index(k) for k in range(len(axes))]
    parts = parts.transpose(*back, *range(len(axes), parts.ndim))
    return parts.reshape(-1, *value.shape)


def gather_axes(value, axes, order, dim):
    return in_order(stacked_from(value, axes, order), dim)


def sent_to_all(value, axis):
    length = lax.axis_size(axis)
    return lax.all_to_all(
        jnp.broadcast_to(value[None], (length, *value.shape)), axis, 0, 0, tiled=True
    )


def taken_together(value, axis):
    return sent_to_all(value, axis).astype(jnp.float32).sum(axis=0)


def joined_by_halves(pieces, combine):
    while len(jax.tree.leaves(pieces)[0]) > 1:
        pieces = jax.vmap(combine)(*(pieces[side::2] for side in (0, 1)))
    return pieces[0]


def carried_in(value, axis, combine, identity):
    length, index = (lax.axis_size(axis), lax.axis_index(axis))
    passed = jnp.arange(length) < index

    def kept(part, zero, own):
        part = jnp.where(
            passed.reshape(-1, *(1 for _ in own.shape)), part, jnp.asarray(zero, own.dtype)
        )
        return part

    pieces = sent_to_all(value, axis)
    return joined_by_halves(kept(pieces, identity, value), combine)


def unpack_codes(packed_words):
    shifts = 2 * jnp.arange(16)
    code_vals = jnp.bitwise_and(jnp.right_shift(packed_words[..., None, :], shifts[:, None]), 3)
    word_shape = packed_words.shape
    return code_vals.reshape(word_shape[:-2] + (word_shape[-2] * 16, word_shape[-1])).astype(
        jnp.float32
    )


def attend_one(request_data):
    (
        query_heads,
        key_new,
        value_new,
        key_words,
        key_step,
        key_offset,
        value_words,
        value_step,
        value_offset,
        seq_length,
    ) = request_data
    kv_heads, head_dim = key_new.shape
    token_group = key_words.shape[1] * 16 // key_step.shape[1]
    keys_deq = unpack_codes(key_words) * jnp.repeat(
        key_step.astype(jnp.float32), token_group, axis=1
    )
    keys_deq = (keys_deq + jnp.repeat(key_offset.astype(jnp.float32), token_group, axis=1)).astype(
        jnp.bfloat16
    )
    values_deq = (
        unpack_codes(value_words) * value_step.astype(jnp.float32)[:, :, None]
        + value_offset.astype(jnp.float32)[:, :, None]
    )
    values_deq = values_deq.astype(jnp.bfloat16)
    grouped = query_heads.reshape(kv_heads, -1, head_dim)
    inv_scale = 1.0 / math.sqrt(head_dim)
    scores = (
        jnp.einsum("kgd,kld->kgl", grouped, keys_deq, preferred_element_type=jnp.float32)
        * inv_scale
    )
    own_score = (
        jnp.einsum("kgd,kd->kg", grouped, key_new, preferred_element_type=jnp.float32) * inv_scale
    )
    usable = jnp.arange(keys_deq.shape[1]) < seq_length
    scores = jnp.where(usable, scores, -jnp.inf)
    highest = jnp.maximum(jnp.max(scores, axis=2), own_score)
    weights = jnp.exp(scores - highest[:, :, None])
    own_weight = jnp.exp(own_score - highest)
    totals = jnp.sum(weights, axis=2) + own_weight
    weights = (weights / totals[:, :, None]).astype(jnp.bfloat16)
    own_weight = (own_weight / totals).astype(jnp.bfloat16)
    result = jnp.einsum("kgl,kld->kgd", weights, values_deq, preferred_element_type=jnp.float32)
    result = (
        result
        + own_weight.astype(jnp.float32)[:, :, None] * value_new.astype(jnp.float32)[:, None, :]
    )
    return result.reshape(-1).astype(jnp.bfloat16)


def expert_ffn(packed_rows, w_gate, w_up, w_down, tensor_sum):
    gate_sum = jnp.dot(packed_rows, w_gate[0], preferred_element_type=jnp.float32)
    up_sum = jnp.dot(packed_rows, w_up[0], preferred_element_type=jnp.float32)
    gate_sum, up_sum = tensor_sum(gate_sum, up_sum)
    activated = (jax.nn.silu(gate_sum) * up_sum).astype(jnp.bfloat16)
    return jnp.dot(activated, w_down[0], preferred_element_type=jnp.float32).astype(jnp.bfloat16)


def add_counts(earlier, later):
    return earlier + later


def shards(
    queries,
    new_keys,
    new_values,
    key_codes,
    key_scale,
    key_zero,
    value_codes,
    value_scale,
    value_zero,
    lengths,
    out_weight,
    residual,
    norm_gain,
    expert_ids,
    route_weights,
    capacity,
    w_gate,
    w_up,
    w_down,
):
    attended = lax.map(
        attend_one,
        (
            queries,
            new_keys,
            new_values,
            key_codes,
            key_scale,
            key_zero,
            value_codes,
            value_scale,
            value_zero,
            lengths,
        ),
    )
    partial_sum = jnp.dot(
        attended,
        gather_axes(out_weight, ("ep", "sub"), (0, 1), 1),
        preferred_element_type=jnp.float32,
    )
    quarter = residual.shape[1]
    tp_index = lax.axis_index("tp")
    own_cols = lax.dynamic_slice_in_dim(
        partial_sum, tp_index * quarter, quarter, 1
    ) + residual.astype(jnp.float32)
    placed = lax.dynamic_update_slice_in_dim(partial_sum, own_cols, tp_index * quarter, 1)
    hidden_full = taken_together(placed.astype(jnp.bfloat16), "tp").astype(jnp.float32)
    hidden_state = lax.dynamic_slice_in_dim(hidden_full, tp_index * quarter, quarter, 1)
    mean_square = jnp.mean(hidden_full * hidden_full, axis=1, keepdims=True)
    normed = (hidden_state * lax.rsqrt(mean_square + EPS) * norm_gain.astype(jnp.float32)).astype(
        jnp.bfloat16
    )
    requests, top_count = expert_ids.shape
    experts_all = capacity.shape[0]
    slot_rows = min(requests, max(2, 5 * requests * top_count // (2 * experts_all)))
    chosen = (expert_ids[:, :, None] == jnp.arange(experts_all, dtype=jnp.int32)).astype(jnp.int32)
    is_named = jnp.sum(chosen, axis=1)
    local_rank = jnp.cumsum(is_named, axis=0) - is_named
    counts = jnp.sum(is_named, axis=0)
    raw_weight = route_weights.astype(jnp.float32)
    shares = raw_weight / jnp.sum(raw_weight, axis=1, keepdims=True)
    weight_per = jnp.sum(chosen.astype(jnp.float32) * shares[:, :, None], axis=1)
    slot_ids = jnp.arange(slot_rows, dtype=jnp.int32)
    at_slot = (local_rank[:, :, None] == slot_ids) & (is_named[:, :, None] > 0)
    offsets = carried_in(counts, ("ep", "sub"), add_counts, jnp.zeros_like(counts))
    kept_rows = offsets[None, :] + local_rank < capacity[None, :]
    send_map = (at_slot & kept_rows[:, :, None]).astype(jnp.bfloat16).reshape(requests, -1)
    outgoing = jnp.dot(send_map.T, normed, preferred_element_type=jnp.float32).astype(jnp.bfloat16)
    outgoing = outgoing.reshape(experts_all, slot_rows, quarter)

    def slot_sums(gate_sum, up_sum):
        return (
            taken_together(gate_sum.astype(jnp.bfloat16), "tp").astype(jnp.float32),
            taken_together(up_sum.astype(jnp.bfloat16), "tp").astype(jnp.float32),
        )

    received = lax.all_to_all(outgoing, ("ep", "sub"), split_axis=0, concat_axis=0, tiled=True)
    source_count, item_count, width = received.shape
    expert_out = expert_ffn(received.reshape(-1, width), w_gate, w_up, w_down, slot_sums)
    returned = lax.all_to_all(
        expert_out.reshape(source_count, item_count, width),
        ("ep", "sub"),
        split_axis=0,
        concat_axis=0,
        tiled=True,
    )
    combine_map = (at_slot.astype(jnp.float32) * weight_per[:, :, None]).reshape(requests, -1)
    moe = jnp.dot(combine_map, returned.reshape(-1, quarter).astype(jnp.float32))
    return (hidden_state + moe).astype(jnp.bfloat16)


def solution(mesh):
    return jax.shard_map(
        shards,
        mesh=mesh,
        in_specs=(
            P(("groups", "ep", "sub"), "tp", None),
            P(("groups", "ep", "sub"), "tp", None),
            P(("groups", "ep", "sub"), "tp", None),
            P(("groups", "ep", "sub"), "tp", None, None),
            P(("groups", "ep", "sub"), "tp", None, None),
            P(("groups", "ep", "sub"), "tp", None, None),
            P(("groups", "ep", "sub"), "tp", None, None),
            P(("groups", "ep", "sub"), "tp", None),
            P(("groups", "ep", "sub"), "tp", None),
            P(("groups", "ep", "sub")),
            P("tp", ("ep", "sub")),
            P(("groups", "ep", "sub"), "tp"),
            P("tp"),
            P(("groups", "ep", "sub"), None),
            P(("groups", "ep", "sub"), None),
            P("groups"),
            P(("ep", "sub"), "tp", None),
            P(("ep", "sub"), "tp", None),
            P(("ep", "sub"), None, "tp"),
        ),
        out_specs=P(("groups", "ep", "sub"), "tp"),
        check_vma=False,
    )
```

profile of v0, /device:TPU:33, one launch (start us, length us, event | category | flops | bytes accessed | tf_op | source)
XLA Modules:
  0.0 389.5 jit_solution(17828715721910761921)
XLA Ops:
  8.7 47.4 %all-to-all-start.1 = ((s32[64,1,64]{2,1,0:T(1,128)}), s32[64,1,64]{2,1,0:T(1,128)S(1)}, u32[]{:S(2)}, u32[]{:S(2)}) async-start(s32[64,1,64]{2,1,0:T(1,128)} %broadcast_in_dim.47), calls=%async_computation.1 | async-start | bytes 65536 | tf_op jit(solution)/shard_map/all_to_all | solution.py:33
  56.4 99.8 %all-gather.5.cloned.1.call-done = bf16[65536,32]{0,1:T(8,128)(2,1)} async-done(((bf16[2048,32]{0,1:T(8,128)(2,1)}), bf16[65536,32]{0,1:T(8,128)(2,1)}) %all-gather.5.cloned.1.call-update) | async-done | bytes 4194320 | tf_op jit(solution)/shard_map/all_gather | solution.py:20
  156.2 6.5 %copy.72 = bf16[4,8,32,2048]{3,2,1,0:T(8,128)(2,1)} copy(bf16[4,8,32,2048]{3,1,2,0:T(8,128)(2,1)} %bitcast.165) | data formatting | bytes 8388608
  162.8 55.4 %while.10 = (s32[]{:T(128)}, bf16[8,2048]{1,0:T(8,128)(2,1)S(1)}, s32[8]{0:T(128)S(1)}, bf16[8,16,128]{2,1,0:T(8,128)(2,1)}, s32[8,1,8,128]{3,2,1,0:T(8,128)}, /...) while((s32[]{:T(128)}, bf16[8,2048]{1,0:T(8,128)(2,1)S(1)}, ...), condition=%wide.region_3.4_spmd, body=%wide.region_0.3_spmd.sunk | while | flops 1273442 | bytes 359669 | solution.py:155
  167.4 0.9 fusion.81
  168.4 0.8 fusion.83
  174.3 0.9 fusion.81
  175.3 0.8 fusion.83
  181.2 0.9 fusion.81
  182.2 0.8 fusion.83
  188.1 0.9 fusion.81
  189.1 0.8 fusion.83
  195.1 0.9 fusion.81
  196.0 0.8 fusion.83
  202.0 0.9 fusion.81
  203.0 0.8 fusion.83
  209.0 0.9 fusion.81
  215.9 0.9 fusion.81
  218.8 11.2 %copy.59 = bf16[32,2,2048,32]{2,3,1,0:T(8,128)(2,1)} copy(bf16[32,2,2048,32]{2,0,1,3:T(8,128)(2,1)} %bitcast.163) | data formatting | bytes 16777216 | tf_op jit(solution)/shard_map/transpose | solution.py:23
  230.0 5.7 %fusion.56 = f32[8,2048]{1,0:T(8,128)S(1)} fusion(bf16[8,2048]{1,0:T(8,128)(2,1)S(1)} %get-tuple-element.67, bf16[2048,2048]{0,1:T(8,128)(2,1)} %bitcast.161), kind=kOutput, calls=%fused_computation.100 | convolution fusion | flops 67108864 | bytes 8486912 | tf_op jit(solution)/shard_map/dot_general | solution.py:170
  236.5 3.4 all-to-all-start
  240.4 4.3 %all-to-all-done = bf16[4,8,2048]{2,1,0:T(8,128)(2,1)S(1)} async-done(((bf16[4,8,2048]{2,1,0:T(8,128)(2,1)}), bf16[4,8,2048]{2,1,0:T(8,128)(2,1)S(1)}, u32[]{:S(2)}, u32[]{:S(2)}) %all-to-all-start) | async-done | bytes 131104 | tf_op jit(solution)/shard_map/all_to_all | solution.py:33
  245.2 65.2 %all_to_all.34 = bf16[64,2,512]{2,1,0:T(2,128)(2,1)S(1)} all-to-all(bf16[64,2,512]{2,1,0:T(2,128)(2,1)S(1)} %reshape.345), channel_id=1, replica_groups=mesh['groups'=2,'ep'=32,'tp'=4,'sub'=2] {'ep','sub'}, dimensions={0} | all-to-all | bytes 262144 | tf_op jit(solution)/shard_map/all_to_all | solution.py:211
  310.8 0.9 broadcast_in_dim.49
  311.7 3.6 all-to-all-start.3
  315.6 9.9 %all-to-all-done.3 = bf16[4,128,768]{2,1,0:T(8,128)(2,1)S(1)} async-done(((bf16[4,128,768]{2,1,0:T(8,128)(2,1)}), bf16[4,128,768]{2,1,0:T(8,128)(2,1)S(1)}, u32[]{:S(2)}, u32[]{:S(2)}) %all-to-all-start.3) | async-done | bytes 786464 | tf_op jit(solution)/shard_map/all_to_all | solution.py:33
  325.5 0.9 broadcast_in_dim.50
  326.5 3.6 all-to-all-start.4
  330.2 9.0 %all-to-all-done.4 = bf16[4,128,768]{2,1,0:T(8,128)(2,1)S(1)} async-done(((bf16[4,128,768]{2,1,0:T(8,128)(2,1)}), bf16[4,128,768]{2,1,0:T(8,128)(2,1)S(1)}, u32[]{:S(2)}, u32[]{:S(2)}) %all-to-all-start.4) | async-done | bytes 786464 | tf_op jit(solution)/shard_map/all_to_all | solution.py:33
  339.3 1.4 convolution_convert_fusion.2
  341.4 10.4 %all-to-all-start.5 = ((bf16[64,2,512]{2,1,0:T(2,128)(2,1)}), bf16[64,2,512]{2,1,0:T(2,128)(2,1)S(1)}, u32[]{:S(2)}, u32[]{:S(2)}) async-start(bf16[64,2,512]{2,1,0:T(2,128)(2,1)} %reshape.347), calls=%async_computation.5 | async-start | bytes 262144 | tf_op jit(solution)/shard_map/all_to_all | solution.py:214
  352.4 29.5 %all-to-all-done.5 = bf16[64,2,512]{2,1,0:T(2,128)(2,1)S(1)} async-done(((bf16[64,2,512]{2,1,0:T(2,128)(2,1)}), bf16[64,2,512]{2,1,0:T(2,128)(2,1)S(1)}, u32[]{:S(2)}, u32[]{:S(2)}) %all-to-all-start.5) | async-done | bytes 131104 | tf_op jit(solution)/shard_map/all_to_all | solution.py:214
  (230 shorter events, 49.7 us)
Async XLA Ops:
  6.5 303.9 %copy-start = (bf16[1,512,768]{2,1,0:T(8,128)(2,1)S(1)}, bf16[1,512,768]{2,1,0:T(8,128)(2,1)}, u32[]{:S(2)}) copy-start(bf16[1,512,768]{2,1,0:T(8,128)(2,1)} %param.37) | copy-start | bytes 2359300
  6.6 156.3 %copy-start.7 = (s32[8]{0:T(128)S(1)}, s32[8]{0:T(128)}, u32[]{:S(2)}) copy-start(s32[8]{0:T(128)} %param.30) | copy-start | bytes 100
  6.6 211.7 %copy-start.5 = (bf16[512]{0:T(512)(128)(2,1)S(1)}, bf16[512]{0:T(512)(128)(2,1)}, u32[]{:S(2)}) copy-start(bf16[512]{0:T(512)(128)(2,1)} %param.33) | copy-start | bytes 3076
  6.6 149.7 %all-gather.5.cloned.1.call-start = ((), (), s32[]{:S(2)}) async-start(), calls=%async_computation.6 | async-start | bytes 4325376 | tf_op jit(solution)/shard_map/all_gather | solution.py:20
  8.7 209.7 %all-to-all-start.1 = ((s32[64,1,64]{2,1,0:T(1,128)}), s32[64,1,64]{2,1,0:T(1,128)S(1)}, u32[]{:S(2)}, u32[]{:S(2)}) async-start(s32[64,1,64]{2,1,0:T(1,128)} %broadcast_in_dim.47), calls=%async_computation.1 | async-start | bytes 65536 | tf_op jit(solution)/shard_map/all_to_all | solution.py:33
  56.2 162.6 %all-gather.7.cloned.1.call-start = ((), (), s32[]{:S(2)}) async-start(), calls=%async_computation.7 | async-start | bytes 12582912 | tf_op jit(solution)/shard_map/all_gather | solution.py:20
  230.0 5.7 %copy-start.4 = (bf16[8,512]{1,0:T(8,128)(2,1)S(1)}, bf16[8,512]{1,0:T(8,128)(2,1)}, u32[]{:S(2)}) copy-start(bf16[8,512]{1,0:T(8,128)(2,1)} %param.32) | copy-start | bytes 24580
  230.0 9.9 %copy-start.6 = (s32[64]{0:T(128)S(1)}, s32[64]{0:T(128)}, u32[]{:S(2)}) copy-start(s32[64]{0:T(128)} %param.36) | copy-start | bytes 772
  230.0 85.3 %copy-start.1 = (bf16[1,512,768]{2,1,0:T(8,128)(2,1)S(1)}, bf16[1,512,768]{2,1,0:T(8,128)(2,1)}, u32[]{:S(2)}) copy-start(bf16[1,512,768]{2,1,0:T(8,128)(2,1)} %param.38) | copy-start | bytes 2359300
  235.8 116.1 %copy-start.2 = (s32[8,8]{1,0:T(8,128)S(1)}, s32[8,8]{1,0:T(8,128)}, u32[]{:S(2)}) copy-start(s32[8,8]{1,0:T(8,128)} %param.35) | copy-start | bytes 772
  235.8 116.3 %copy-start.3 = (s32[8,8]{1,0:T(8,128)S(1)}, s32[8,8]{1,0:T(8,128)}, u32[]{:S(2)}) copy-start(s32[8,8]{1,0:T(8,128)} %param.34) | copy-start | bytes 772
  236.5 8.3 %all-to-all-start = ((bf16[4,8,2048]{2,1,0:T(8,128)(2,1)}), bf16[4,8,2048]{2,1,0:T(8,128)(2,1)S(1)}, u32[]{:S(2)}, u32[]{:S(2)}) async-start(bf16[4,8,2048]{2,1,0:T(8,128)(2,1)} %broadcast_in_dim.45), calls=%async_computation | async-start | bytes 262144 | tf_op jit(solution)/shard_map/all_to_all | solution.py:33
  311.7 13.8 %all-to-all-start.3 = ((bf16[4,128,768]{2,1,0:T(8,128)(2,1)}), bf16[4,128,768]{2,1,0:T(8,128)(2,1)S(1)}, u32[]{:S(2)}, u32[]{:S(2)}) async-start(bf16[4,128,768]{2,1,0:T(8,128)(2,1)} %broadcast_in_dim.49), calls=%async_computation.3 | async-start | bytes 1572864 | tf_op jit(solution)/shard_map/all_to_all | solution.py:33
  326.5 12.7 %all-to-all-start.4 = ((bf16[4,128,768]{2,1,0:T(8,128)(2,1)}), bf16[4,128,768]{2,1,0:T(8,128)(2,1)S(1)}, u32[]{:S(2)}, u32[]{:S(2)}) async-start(bf16[4,128,768]{2,1,0:T(8,128)(2,1)} %broadcast_in_dim.50), calls=%async_computation.4 | async-start | bytes 1572864 | tf_op jit(solution)/shard_map/all_to_all | solution.py:33
  341.4 40.4 %all-to-all-start.5 = ((bf16[64,2,512]{2,1,0:T(2,128)(2,1)}), bf16[64,2,512]{2,1,0:T(2,128)(2,1)S(1)}, u32[]{:S(2)}, u32[]{:S(2)}) async-start(bf16[64,2,512]{2,1,0:T(2,128)(2,1)} %reshape.347), calls=%async_computation.5 | async-start | bytes 262144 | tf_op jit(solution)/shard_map/all_to_all | solution.py:214
Sparse Core Ops, SparseCore 0:
  9.4 146.7 all-gather.4
  162.9 51.8 all-gather.6
where the time goes:
time: 392 us; the launch traced here: 390 us
  waiting for transfers between devices  153 us (39%)
  starting transfers between devices  68.7 us (18%)
  blocking collectives  65.2 us (17%)
  local copies, waits for them, and re-layouts  36.1 us (9%)
  other arithmetic  27.3 us (7%)
  matrix products  24.5 us (6%)
  between operations  13.7 us (3%)
    all_gather x2, waiting for transfers between devices, stacked_from(): parts = lax.all_gather(parts, axes[k])  99.8 us
    all_to_all x1, blocking collectives, shards(): lax.all_to_all(outgoing, ('ep', 'sub'), split_axis=0, concat_axis=0, tile...  65.2 us
    all_to_all x4, starting transfers between devices, sent_to_all(): lax.all_to_all(jnp.broadcast_to(value[None], (length, *value.shape)), axi...  58 us
    all_to_all x1, waiting for transfers between devices, shards(): lax.all_to_all(expert_out.reshape(source_count, item_count, width), ('ep'...  29.5 us
    all_to_all x4, waiting for transfers between devices, sent_to_all(): lax.all_to_all(jnp.broadcast_to(value[None], (length, *value.shape)), axi...  23.3 us
    transpose x1, local copies, waits for them, and re-layouts, stacked_from(): parts = parts.transpose(*back, *range(len(axes), parts.ndim))  11.2 us
    all_to_all x1, starting transfers between devices, shards(): lax.all_to_all(expert_out.reshape(source_count, item_count, width), ('ep'...  10.4 us
  transfers between devices with their start and end apart: 7, of which 5 were waited for; matrix products, arithmetic and copies ran while one was open for 17% of the time, Pallas kernels for 0%

commit v1 on v0

v1 whole, which is shorter than its diff:
```python
import functools
import math

import jax
import jax.numpy as jnp
from jax import lax
from jax.experimental import pallas as pl
from jax.experimental.pallas import tpu as pltpu
from jax.sharding import PartitionSpec as P

EPS = 1e-06
PIECES = 4
SLOTS = 2
RANKS = 32
MESH = pl.DeviceIdType.MESH
F32, BF16, I32 = jnp.float32, jnp.bfloat16, jnp.int32


def nt_dot(a, b):
    return lax.dot_general(a, b, (((1,), (1,)), ((), ())), preferred_element_type=F32)


def nn_dot(a, b):
    return jnp.dot(a, b, preferred_element_type=F32)


def kernel(
    q_ref, nk_ref, nv_ref, kc_ref, ks_ref, kz_ref, vc_ref, vs_ref, vz_ref, len_ref,
    w_ref, res_ref, gain_ref, ids_ref, rw_ref, cap_ref, wg_hbm, wu_hbm, wd_hbm,
    out_ref,
    blocks, counts, att, att_rows, att_both, att_bf, row_f32, proj, rs_send, rs_recv,
    pick_t, comb_t, place, d_send, d_recv, r_send, r_recv,
    wg, wu, wd, g_send, g_recv, act,
    own_sem, w_sem, ring_send, ring_recv, cnt_send, cnt_recv,
    att_sem, cpair_sem, rs_sem, dd_sem, rr_sem, gg_sem, aa_sem,
):
    nz, ntp, nc = lax.axis_size("ep"), lax.axis_size("tp"), lax.axis_size("sub")
    z, tp, sub = lax.axis_index("ep"), lax.axis_index("tp"), lax.axis_index("sub")
    nr = nz * nc
    me = z * nc + sub
    half = nz // 2
    up, down = lax.rem(z + 1, nz), lax.rem(z + nz - 1, nz)
    other = 1 - sub
    ngrp = ntp * nc
    mine = tp * nc + sub
    reqs, heads, hd = q_ref.shape
    cols = blocks.shape[2]
    rows_w = w_ref.shape[1]
    piece = rows_w // PIECES
    quarter = res_ref.shape[1]
    lt = quarter // 128
    msg = SLOTS * lt
    lanes = nr * msg
    inv_scale = 1.0 / math.sqrt(hd)

    own_copies = [
        pltpu.make_async_copy(
            w_ref.at[:, pl.ds(p * piece, piece)], blocks.at[z, p], own_sem.at[p]
        )
        for p in range(PIECES)
    ]
    w_copies = [
        pltpu.make_async_copy(src, dst, w_sem.at[i])
        for i, (src, dst) in enumerate(((wg_hbm, wg), (wu_hbm, wu), (wd_hbm, wd)))
    ]
    for copy in own_copies:
        copy.start()

    barrier = pltpu.get_barrier_semaphore()
    for near in (up, down):
        pl.semaphore_signal(barrier, 1, device_id={"ep": near}, device_id_type=MESH)

    def group_member(k):
        there = lax.rem(mine + k, ngrp)
        return there // nc, lax.rem(there, nc)

    for k in range(1, ngrp):
        there_tp, there_sub = group_member(k)
        pl.semaphore_signal(
            barrier, 1, device_id={"tp": there_tp, "sub": there_sub}, device_id_type=MESH
        )

    ids = ids_ref[...]
    lane128 = lax.broadcasted_iota(I32, (reqs, 128), 1)
    named = jnp.zeros((reqs, 128), F32)
    for k in range(ids.shape[1]):
        named = named + (ids[:, k : k + 1] == lane128).astype(F32)
    counts[sub, z] = jnp.sum(named, axis=0, keepdims=True)

    pl.semaphore_wait(barrier, 2 + ngrp - 1)

    def block_copy(way, step, p):
        at = lax.rem(z - step + nz, nz) if way == 0 else lax.rem(z + step, nz)
        return pltpu.make_async_remote_copy(
            src_ref=blocks.at[at, p],
            dst_ref=blocks.at[at, p],
            send_sem=ring_send.at[way, step, p],
            recv_sem=ring_recv.at[way, step, p],
            device_id={"ep": up if way == 0 else down},
            device_id_type=MESH,
        )

    def count_copy(way, step):
        at = lax.rem(z - step + nz, nz) if way == 0 else lax.rem(z + step, nz)
        return pltpu.make_async_remote_copy(
            src_ref=counts.at[sub, at],
            dst_ref=counts.at[sub, at],
            send_sem=cnt_send.at[way, step],
            recv_sem=cnt_recv.at[way, step],
            device_id={"ep": up if way == 0 else down},
            device_id_type=MESH,
        )

    for p in range(PIECES):
        own_copies[p].wait()
        for way in (0, 1):
            block_copy(way, 0, p).start()
    for way in (0, 1):
        count_copy(way, 0).start()
    for copy in w_copies:
        copy.start()

    def pass_on(step, p):
        for way in (0, 1):
            block_copy(way, step - 1, p).wait_recv()
            block_copy(way, step, p).start()

    def pass_counts(step):
        for way in (0, 1):
            count_copy(way, step - 1).wait_recv()
            count_copy(way, step).start()

    def attend_scores(b):
        sixteen = 2 * lax.broadcasted_iota(I32, (16, hd), 0)
        words = kc_ref[b]
        steps = ks_ref[b].astype(F32)
        zeros = kz_ref[b].astype(F32)
        per_group = words.shape[0] // steps.shape[0]
        keys = []
        for w in range(words.shape[0]):
            codes = jnp.bitwise_and(jnp.right_shift(words[w : w + 1, :], sixteen), 3)
            g = w // per_group
            keys.append(codes.astype(F32) * steps[g : g + 1, :] + zeros[g : g + 1, :])
        keys = jnp.concatenate(keys, axis=0).astype(BF16)
        q = q_ref[b]
        scores = nt_dot(q, keys) * inv_scale
        own = jnp.sum(q.astype(F32) * row_f32[0, b], axis=1, keepdims=True) * inv_scale
        usable = lax.broadcasted_iota(I32, scores.shape, 1) < len_ref[b]
        scores = jnp.where(usable, scores, -jnp.inf)
        highest = jnp.maximum(jnp.max(scores, axis=1, keepdims=True), own)
        weights = jnp.exp(scores - highest)
        own = jnp.exp(own - highest)
        totals = jnp.sum(weights, axis=1, keepdims=True) + own
        att[b, 0] = (weights / totals).astype(BF16).astype(F32)
        att[b, 1] = jnp.broadcast_to((own / totals).astype(BF16).astype(F32), (heads, hd))

    def attend_values(b):
        sixteen = 2 * lax.broadcasted_iota(I32, (16, hd), 0)
        words = vc_ref[b]
        values = []
        for w in range(words.shape[0]):
            codes = jnp.bitwise_and(jnp.right_shift(words[w : w + 1, :], sixteen), 3)
            values.append(codes.astype(F32))
        values = jnp.concatenate(values, axis=0).astype(BF16)
        weights = att[b, 0]
        scaled = weights * row_f32[2, b]
        high = scaled.astype(BF16)
        low = (scaled - high.astype(F32)).astype(BF16)
        summed = nn_dot(jnp.concatenate([high, low], axis=0), values)
        offset = jnp.sum(weights * row_f32[3, b], axis=1, keepdims=True)
        result = summed[:heads] + summed[heads:] + offset + att[b, 1] * row_f32[1, b]
        att_rows[pl.ds(pl.multiple_of(b * heads, heads), heads), :] = result.astype(BF16).astype(F32)

    for i, ref in enumerate((nk_ref, nv_ref, vs_ref, vz_ref)):
        rows = ref[...].astype(F32)
        for b in range(reqs):
            row_f32[i, b] = rows[b : b + 1, :]

    n_att = max(1, half // 4)
    per_step = reqs // n_att

    def attention_step(step, _):
        first = (step - 1) * per_step
        for p in range(PIECES):
            pass_on(step, p)
            if p == 0:
                pass_counts(step)
                for b in range((per_step + 1) // 2):
                    attend_scores(first + b)
            elif p == 1:
                for b in range((per_step + 1) // 2, per_step):
                    attend_scores(first + b)
            elif p == 2:
                for b in range((per_step + 1) // 2):
                    attend_values(first + b)
            else:
                for b in range((per_step + 1) // 2, per_step):
                    attend_values(first + b)
        return 0

    lax.fori_loop(1, n_att + 1, attention_step, 0)

    for h in range(heads):
        att_both[sub, :, h * hd : (h + 1) * hd] = att_rows[pl.ds(h, reqs, stride=heads), :]
    att_copy = pltpu.make_async_remote_copy(
        src_ref=att_both.at[sub],
        dst_ref=att_both.at[sub],
        send_sem=att_sem.at[0],
        recv_sem=att_sem.at[1],
        device_id={"sub": other},
        device_id_type=MESH,
    )
    att_copy.start()

    lane = lax.broadcasted_iota(I32, (reqs, lanes), 1)
    expert_at = lane // msg
    slot_at = lax.rem(lane, msg) // lt
    tile_at = lax.rem(lane, lt)
    raw = rw_ref[...].astype(F32)
    shares = raw / jnp.sum(raw, axis=1, keepdims=True)
    named = jnp.zeros((reqs, lanes), F32)
    weight = jnp.zeros((reqs, lanes), F32)
    for k in range(ids.shape[1]):
        hit = ids[:, k : k + 1] == expert_at
        named = jnp.where(hit, 1.0, named)
        weight = jnp.where(hit, shares[:, k : k + 1], weight)
    running = jnp.zeros((1, lanes), F32)
    ranks = []
    for b in range(reqs):
        ranks.append(running)
        running = running + named[b : b + 1, :]
    local_rank = jnp.concatenate(ranks, axis=0)
    chosen = jnp.where(local_rank == slot_at.astype(F32), named, 0.0)
    weight = weight * chosen
    high = weight.astype(BF16).astype(F32)
    low = weight - high
    for l in range(lt):
        here = tile_at == l
        pick_t[l * reqs : (l + 1) * reqs, :] = jnp.where(here, chosen, 0.0)
        comb_t[l * reqs : (l + 1) * reqs, :] = jnp.where(here, high, 0.0).astype(BF16)
        comb_t[(lt + l) * reqs : (lt + l + 1) * reqs, :] = jnp.where(here, low, 0.0).astype(BF16)
    pick = jnp.transpose(pick_t[...]).astype(BF16)

    att_copy.wait()
    both = att_both[...].reshape(nc * reqs, rows_w)
    att_bf[...] = both.astype(BF16)

    def project(at):
        total = nt_dot(att_bf[:, 0:piece], blocks[at, 0])
        for p in range(1, PIECES):
            total += nt_dot(att_bf[:, p * piece : (p + 1) * piece], blocks[at, p])
        proj[at] = total

    def behind(distance):
        return lax.rem(z - distance + nz, nz)

    def ahead(distance):
        return lax.rem(z + distance, nz)

    def catch_up_step(step, _):
        for p in range(PIECES):
            pass_on(step, p)
            if p == 0:
                pass_counts(step)
                project(behind(step - 1 - n_att))
            elif p == 1:
                project(ahead(step - 1 - n_att))
            elif p == 2:
                project(behind(step - 1))
            else:
                project(ahead(step - 1))
        return 0

    def projection_step(step, _):
        for p in range(PIECES):
            pass_on(step, p)
            if p == 0:
                pass_counts(step)
            elif p == 1:
                project(behind(step - 1))
            elif p == 2:
                project(ahead(step - 1))
        return 0

    lax.fori_loop(n_att + 1, 2 * n_att + 1, catch_up_step, 0)
    lax.fori_loop(2 * n_att + 1, half - 1, projection_step, 0)

    last = half - 1
    for p in range(PIECES):
        for way in (0, 1):
            block_copy(way, last - 1, p).wait_recv()
            if (p < PIECES // 2) == (way == 0):
                block_copy(way, last, p).start()
        if p == 0:
            for way in (0, 1):
                count_copy(way, last - 1).wait_recv()
            count_copy(0, last).start()
        elif p == 1:
            project(behind(last - 1))
        elif p == 2:
            project(ahead(last - 1))
    project(behind(last))
    project(ahead(last))
    count_copy(0, last).wait_recv()
    count_pair = pltpu.make_async_remote_copy(
        src_ref=counts.at[sub],
        dst_ref=counts.at[sub],
        send_sem=cpair_sem.at[0],
        recv_sem=cpair_sem.at[1],
        device_id={"sub": other},
        device_id_type=MESH,
    )
    count_pair.start()
    for p in range(PIECES):
        block_copy(0 if p < PIECES // 2 else 1, last, p).wait_recv()
    project(ahead(half))

    per_quarter = nz // ntp
    for t in range(ntp):
        part = jnp.concatenate([proj[t * per_quarter + i] for i in range(per_quarter)], axis=1)
        for c in range(nc):
            rs_send[t * nc + c] = part[c * reqs : (c + 1) * reqs, :].astype(BF16)

    def rs_copy(k):
        there_tp, there_sub = group_member(k)
        return pltpu.make_async_remote_copy(
            src_ref=rs_send.at[lax.rem(mine + k, ngrp)],
            dst_ref=rs_recv.at[k - 1],
            send_sem=rs_sem.at[0, k],
            recv_sem=rs_sem.at[1, k],
            device_id={"tp": there_tp, "sub": there_sub},
            device_id_type=MESH,
        )

    for k in range(1, ngrp):
        rs_copy(k).start()
    sums = [rs_send[mine].astype(F32), None]
    for k in range(1, ngrp):
        rs_copy(k).wait_recv()
        got = rs_recv[k - 1].astype(F32)
        side = k % nc
        sums[side] = got if sums[side] is None else sums[side] + got
    own_first = sub == 0
    first = jnp.where(own_first, sums[0], sums[1])
    second = jnp.where(own_first, sums[1], sums[0])
    hidden = jnp.concatenate(
        [
            side[:, i * cols : (i + 1) * cols]
            for i in range(per_quarter)
            for side in (first, second)
        ],
        axis=1,
    ) + res_ref[...].astype(F32)

    hidden_bf = hidden.astype(BF16)
    stacked = jnp.concatenate([hidden_bf[:, l * 128 : (l + 1) * 128].astype(F32) for l in range(lt)], axis=0)
    outgoing = nn_dot(pick, stacked.astype(BF16)).astype(BF16)
    d_send[...] = outgoing.reshape(nr, msg, 128)

    def far_first(i):
        return nr // 2 + ((i + 1) // 2) * (2 * lax.rem(i, 2) - 1)

    def d_copy(k):
        there = lax.rem(me + k, nr)
        return pltpu.make_async_remote_copy(
            src_ref=d_send.at[there],
            dst_ref=d_recv.at[k - 1],
            send_sem=dd_sem.at[0],
            recv_sem=dd_sem.at[1],
            device_id={"ep": there // nc, "sub": lax.rem(there, nc)},
            device_id_type=MESH,
        )

    count_pair.wait()

    def d_start(i, _):
        d_copy(far_first(i)).start()
        return 0

    lax.fori_loop(0, nr - 1, d_start, 0)
    d_recv[nr - 1] = d_send[me]

    one_lane = (lax.broadcasted_iota(I32, (8, 128), 1) == me).astype(BF16)
    cnt_rows = [counts[c].reshape(nz, 128).astype(BF16) for c in range(nc)]
    cnt8 = [nt_dot(one_lane, rows).astype(BF16) for rows in cnt_rows]
    col = lax.broadcasted_iota(I32, (nz, lanes), 1)
    source = lax.rem(me + 2 * nr - 1 - col // msg, nr)
    row_z = lax.broadcasted_iota(I32, (nz, lanes), 0)
    before = jnp.zeros((8, lanes), F32)
    here = jnp.zeros((8, lanes), F32)
    for c in range(nc):
        row_id = row_z * nc + c
        before = before + nn_dot(cnt8[c], (row_id < source).astype(F32).astype(BF16))
        here = here + nn_dot(cnt8[c], (row_id == source).astype(F32).astype(BF16))
    lane1 = lax.broadcasted_iota(I32, (1, lanes), 1)
    slot1 = (lax.rem(lane1, msg) // lt).astype(F32)
    tile1 = lax.rem(lane1, lt)
    position = before[0:1] + slot1
    valid = (slot1 < here[0:1]) & (position < cap_ref[me].astype(F32))
    position = jnp.where(valid, position, -1.0)
    rank_at = lax.broadcasted_iota(I32, (RANKS, lanes), 0).astype(F32)
    for l in range(lt):
        hit = (rank_at == position) & (tile1 == l)
        place[l * RANKS : (l + 1) * RANKS, :] = jnp.where(hit, 1.0, 0.0)
    place_bf = place[...].astype(BF16)
    spread_bf = jnp.transpose(place[...]).astype(BF16)
    for copy in w_copies:
        copy.wait()

    pltpu.make_async_copy(d_recv.at[pl.ds(0, nr - 1)], d_recv.at[pl.ds(0, nr - 1)], dd_sem.at[1]).wait()

    packed = nn_dot(place_bf, d_recv[...].reshape(lanes, 128))
    packed = jnp.concatenate([packed[l * RANKS : (l + 1) * RANKS] for l in range(lt)], axis=1)
    squares = jnp.sum(packed * packed, axis=1, keepdims=True)
    gained = (packed * gain_ref[...].astype(F32)).astype(BF16)
    ff = wg.shape[1]
    own_rows = RANKS // ntp
    gate = nn_dot(gained, wg[...])
    upper = nn_dot(gained, wu[...])
    sq_high = squares.astype(BF16).astype(F32)
    on_left = lax.broadcasted_iota(I32, (RANKS, 128), 1) < 64
    sq_both = jnp.where(on_left, sq_high, squares - sq_high)
    for t in range(ntp):
        span = slice(t * own_rows, (t + 1) * own_rows)
        g_send[t, :, 0:ff] = gate[span].astype(BF16)
        g_send[t, :, ff : 2 * ff] = upper[span].astype(BF16)
        g_send[t, :, 2 * ff :] = sq_both[span].astype(BF16)

    def g_copy(k):
        there = lax.rem(tp + k, ntp)
        return pltpu.make_async_remote_copy(
            src_ref=g_send.at[there],
            dst_ref=g_recv.at[k - 1],
            send_sem=gg_sem.at[0, k],
            recv_sem=gg_sem.at[1, k],
            device_id={"tp": there},
            device_id_type=MESH,
        )

    far_tp = sorted(range(1, ntp), key=lambda k: -min(k, ntp - k))
    for k in far_tp:
        g_copy(k).start()
    total = g_send[tp].astype(F32)
    for k in range(1, ntp):
        g_copy(k).wait_recv()
        total = total + g_recv[k - 1].astype(F32)
    square = total[:, 2 * ff : 2 * ff + 1] + total[:, 2 * ff + 64 : 2 * ff + 65]
    scale = lax.rsqrt(square / (quarter * ntp) + EPS)
    gate = total[:, 0:ff] * scale
    upper = total[:, ff : 2 * ff] * scale
    act[tp] = (gate / (1.0 + jnp.exp(-gate)) * upper).astype(BF16)

    def a_copy(k):
        return pltpu.make_async_remote_copy(
            src_ref=act.at[tp],
            dst_ref=act.at[tp],
            send_sem=aa_sem.at[0, k],
            recv_sem=aa_sem.at[1, k],
            device_id={"tp": lax.rem(tp + k, ntp)},
            device_id_type=MESH,
        )

    for k in far_tp:
        a_copy(k).start()
    for k in range(1, ntp):
        a_copy(k).wait_recv()
    activated = jnp.concatenate([act[t].astype(F32) for t in range(ntp)], axis=0).astype(BF16)
    result = nn_dot(activated, wd[...])
    stacked = jnp.concatenate([result[:, l * 128 : (l + 1) * 128] for l in range(lt)], axis=0)
    back = nn_dot(spread_bf, stacked.astype(BF16)).astype(BF16)
    r_send[...] = back.reshape(nr, msg, 128)

    def r_copy(k):
        there = lax.rem(me + nr - k, nr)
        return pltpu.make_async_remote_copy(
            src_ref=r_send.at[k - 1],
            dst_ref=r_recv.at[me],
            send_sem=rr_sem.at[0],
            recv_sem=rr_sem.at[1],
            device_id={"ep": there // nc, "sub": lax.rem(there, nc)},
            device_id_type=MESH,
        )

    def r_start(i, _):
        r_copy(far_first(i)).start()
        return 0

    lax.fori_loop(0, nr - 1, r_start, 0)
    r_recv[me] = r_send[nr - 1]

    def sent(step, _):
        for way in (0, 1):
            for p in range(PIECES):
                block_copy(way, step, p).wait_send()
            count_copy(way, step).wait_send()
        return 0

    lax.fori_loop(0, last, sent, 0)
    for p in range(PIECES):
        block_copy(0 if p < PIECES // 2 else 1, last, p).wait_send()
    count_copy(0, last).wait_send()
    for k in range(1, ngrp):
        rs_copy(k).wait_send()
    for k in range(1, ntp):
        g_copy(k).wait_send()
        a_copy(k).wait_send()
    pltpu.make_async_copy(d_recv.at[pl.ds(0, nr - 1)], d_recv.at[pl.ds(0, nr - 1)], dd_sem.at[0]).wait()

    pltpu.make_async_copy(r_recv.at[pl.ds(0, nr - 1)], r_recv.at[pl.ds(0, nr - 1)], rr_sem.at[1]).wait()
    moe = nn_dot(comb_t[...], r_recv[...].reshape(lanes, 128))
    moe = moe[: lt * reqs] + moe[lt * reqs :]
    moe = jnp.concatenate([moe[l * reqs : (l + 1) * reqs] for l in range(lt)], axis=1)
    out_ref[...] = (hidden + moe).astype(BF16)
    pltpu.make_async_copy(r_send.at[pl.ds(0, nr - 1)], r_send.at[pl.ds(0, nr - 1)], rr_sem.at[0]).wait()


def shards(
    queries, new_keys, new_values, key_codes, key_scale, key_zero, value_codes,
    value_scale, value_zero, lengths, out_weight, residual, norm_gain, expert_ids,
    route_weights, capacity, w_gate, w_up, w_down,
):
    nz, ntp, nc = lax.axis_size("ep"), lax.axis_size("tp"), lax.axis_size("sub")
    nr = nz * nc
    reqs, heads, hd = queries.shape
    rows_w, cols = out_weight.shape
    quarter = residual.shape[1]
    channels, ff = w_gate.shape[1:]
    lt = quarter // 128
    msg = SLOTS * lt
    lanes = nr * msg
    half = nz // 2
    ngrp = ntp * nc
    vmem = pl.BlockSpec(memory_space=pltpu.VMEM)
    smem = pl.BlockSpec(memory_space=pltpu.SMEM)
    hbm = pl.BlockSpec(memory_space=pl.ANY)
    dma = pltpu.SemaphoreType.DMA
    return pl.pallas_call(
        kernel,
        out_shape=jax.ShapeDtypeStruct((reqs, quarter), BF16),
        in_specs=[vmem] * 9 + [smem, hbm] + [vmem] * 4 + [smem] + [hbm] * 3,
        out_specs=vmem,
        scratch_shapes=[
            pltpu.VMEM((nz, PIECES, cols, rows_w // PIECES), BF16),
            pltpu.VMEM((nc, nz, 1, 128), F32),
            pltpu.VMEM((reqs, 2, heads, hd), F32),
            pltpu.VMEM((reqs * heads, hd), F32),
            pltpu.VMEM((nc, reqs, rows_w), F32),
            pltpu.VMEM((nc * reqs, rows_w), BF16),
            pltpu.VMEM((4, reqs, 1, hd), F32),
            pltpu.VMEM((nz, nc * reqs, cols), F32),
            pltpu.VMEM((ngrp, reqs, quarter // nc), BF16),
            pltpu.VMEM((ngrp - 1, reqs, quarter // nc), BF16),
            pltpu.VMEM((lt * reqs, lanes), F32),
            pltpu.VMEM((2 * lt * reqs, lanes), BF16),
            pltpu.VMEM((lt * RANKS, lanes), F32),
            pltpu.VMEM((nr, msg, 128), BF16),
            pltpu.VMEM((nr, msg, 128), BF16),
            pltpu.VMEM((nr, msg, 128), BF16),
            pltpu.VMEM((nr, msg, 128), BF16),
            pltpu.VMEM((channels, ff), BF16),
            pltpu.VMEM((channels, ff), BF16),
            pltpu.VMEM((ff, quarter), BF16),
            pltpu.VMEM((ntp, RANKS // ntp, 2 * ff + 128), BF16),
            pltpu.VMEM((max(1, ntp - 1), RANKS // ntp, 2 * ff + 128), BF16),
            pltpu.VMEM((ntp, RANKS // ntp, ff), BF16),
            dma((PIECES,)),
            dma((3,)),
            dma((2, half, PIECES)),
            dma((2, half, PIECES)),
            dma((2, half)),
            dma((2, half)),
            dma((2,)),
            dma((2,)),
            dma((2, ngrp)),
            dma((2,)),
            dma((2,)),
            dma((2, ntp)),
            dma((2, ntp)),
        ],
        compiler_params=pltpu.CompilerParams(collective_id=0, has_side_effects=True),
        name="decode_moe",
    )(
        queries,
        new_keys.reshape(reqs, hd),
        new_values.reshape(reqs, hd),
        key_codes.reshape(reqs, -1, hd),
        key_scale.reshape(reqs, -1, hd),
        key_zero.reshape(reqs, -1, hd),
        value_codes.reshape(reqs, -1, hd),
        value_scale.reshape(reqs, -1),
        value_zero.reshape(reqs, -1),
        lengths,
        out_weight.T,
        residual,
        norm_gain.reshape(1, quarter),
        expert_ids,
        route_weights,
        capacity,
        w_gate.reshape(channels, ff),
        w_up.reshape(channels, ff),
        w_down.reshape(ff, quarter),
    )


def solution(mesh):
    return jax.shard_map(
        shards,
        mesh=mesh,
        in_specs=(
            P(("groups", "ep", "sub"), "tp", None),
            P(("groups", "ep", "sub"), "tp", None),
            P(("groups", "ep", "sub"), "tp", None),
            P(("groups", "ep", "sub"), "tp", None, None),
            P(("groups", "ep", "sub"), "tp", None, None),
            P(("groups", "ep", "sub"), "tp", None, None),
            P(("groups", "ep", "sub"), "tp", None, None),
            P(("groups", "ep", "sub"), "tp", None),
            P(("groups", "ep", "sub"), "tp", None),
            P(("groups", "ep", "sub")),
            P("tp", ("ep", "sub")),
            P(("groups", "ep", "sub"), "tp"),
            P("tp"),
            P(("groups", "ep", "sub"), None),
            P(("groups", "ep", "sub"), None),
            P("groups"),
            P(("ep", "sub"), "tp", None),
            P(("ep", "sub"), "tp", None),
            P(("ep", "sub"), None, "tp"),
        ),
        out_specs=P(("groups", "ep", "sub"), "tp"),
        check_vma=False,
    )
```

time: 392 us -> 156 us (0.40)
  Pallas kernels: 0 us -> 153 us
  waiting for transfers between devices: 153 us -> 0 us
  starting transfers between devices: 68.7 us -> 0 us
  blocking collectives: 65.2 us -> 0 us
  local copies, waits for them, and re-layouts: 36.1 us -> 2.56 us
  other arithmetic: 27.3 us -> 0 us
  matrix products: 24.5 us -> 0 us
  between operations: 13.7 us -> 0.01 us
    pallas_call x0 -> x1, Pallas kernels: none -> 153 us  [shards(): pl.pallas_call(kernel, out_shape=jax.ShapeDtypeStruct((reqs, quarter), BF...]
    all_gather x2 -> x0, waiting for transfers between devices: 99.8 us -> none  [stacked_from(): parts = lax.all_gather(parts, axes[k])]
    all_to_all x5 -> x0, starting transfers between devices: 68.4 us -> none  [the longest x4 58 us: sent_to_all(): lax.all_to_all(jnp.broadcast_to(value[None], (length, *value.shape)), axi...]
    all_to_all x1 -> x0, blocking collectives: 65.2 us -> none  [shards(): lax.all_to_all(outgoing, ('ep', 'sub'), split_axis=0, concat_axis=0, tile...]
    all_to_all x5 -> x0, waiting for transfers between devices: 52.8 us -> none  [the longest x1 29.5 us: shards(): lax.all_to_all(expert_out.reshape(source_count, item_count, width), ('ep'...]
    dot_general x30 -> x0, matrix products: 24.5 us -> none  [the longest x8 7.55 us: attend_one(): jnp.einsum('kgd,kld->kgl', grouped, keys_deq, preferred_element_type=jnp....]
    convert_element_type x34 -> x0, other arithmetic: 12.9 us -> none  [the longest x8 5.67 us: attend_one(): value_step.astype(jnp.float32)[:, :, None]]
    transpose x1 -> x0, local copies, waits for them, and re-layouts: 11.2 us -> none  [stacked_from(): parts = parts.transpose(*back, *range(len(axes), parts.ndim))]
  transfers between devices with their start and end apart: 7 -> 0, of which waited for: 5 -> 0; matrix products, arithmetic and copies ran while one was open for 17% -> 0% of each run, Pallas kernels for 0% -> 0%
where the time goes in v1:
time: 156 us
  Pallas kernels  153 us (98%)
  local copies, waits for them, and re-layouts  2.56 us (2%)
    pallas_call x1, Pallas kernels, shards(): pl.pallas_call(kernel, out_shape=jax.ShapeDtypeStruct((reqs, quarter), BF...  153 us

profile of v1, /device:TPU:33, one launch (start us, length us, event | category | flops | bytes accessed | tf_op | source)
XLA Modules:
  0.0 156.0 jit_solution(725496594870469821)
XLA Ops:
  0.0 0.0 copy-start
  0.0 0.7 copy-done
  0.7 0.6 reshape.44.gain_ref
  1.3 153.4 %decode_moe.1 = bf16[8,512]{1,0:T(8,128)(2,1)} custom-call(bf16[8,16,128]{2,1,0:T(8,128)(2,1)} %q_ref.1, bf16[8,128]{1,0:T(8,128)(2,1)} %bitcast.20, bf16[8,128]{1,0:T(8,128)(2,1)} %bitcast.21, s32[8,8,128]{2,1,0:T(8,128)} %bitcast.16, bf16[8,4,128]{2,1,0:T(4,128)(2,1)} %bitcast.18, bf16[8,4,128]{2,1,0:T(4,128)(2,1)} %bitcast.19, s32[8,8,128]{2,1,0:T(8,128)} %bitcast.17, ...), custom_call_target="tpu_custom_call" | custom-call | tf_op jit(solution)/shard_map/decode_moe/pallas_call | solution.py:537
  154.7 1.3 copy.21
Async XLA Ops:
  0.0 0.7 copy-start
